TPU v7x, 256 devices: a whole 4x4x8 slice. The times are simulated.
256 devices in a mesh: fsdp: 32 (over z, y), rep: 8 (over x, core).
Axes of the slice: x: 4, y: 4, z: 8, core: 2. Of those that a mesh axis runs over, the one named last changes fastest.
Arguments:
- hidden: bfloat16 [65536, 2048], P(('fsdp', 'rep')), may hold values from -6 to 6
- attn_gain: bfloat16 [2048], P(('fsdp', 'rep')), may hold values from 0.25 to 1.75
- w_query: bfloat16 [2048, 2048], P(('fsdp', 'rep')), as said below
- w_key: bfloat16 [2048, 512], P(('fsdp', 'rep')), as said below
- w_value: bfloat16 [2048, 512], P(('fsdp', 'rep')), may hold values from -0.125 to 0.125
- w_out: bfloat16 [2048, 2048], P(None, ('fsdp', 'rep')), may hold values from -0.125 to 0.125
Outputs:
- mixed: bfloat16 [65536, 2048], P(('fsdp', 'rep'))
Inputs may be any that keep to these rules, and one draw needn't show every extreme that they name: `w_query`: entries of order 2048^(-1/2). `w_key`: entries of order 2048^(-1/2) times a factor up to twenty.
All inputs are finite; a program needn't handle non-finite values.
Results may differ from a plain program's by a relative error of at most 0.012.
The roundings to bfloat16 on the way count: a program that leaves them out, or rounds other values in their place, can miss the bound.
Values may be sent and summed in bfloat16 or wider, within the bound.
A program may use at most 64 MiB of HBM per device.

v0:
```python
import jax
import jax.numpy as jnp
from jax import lax
from jax.sharding import PartitionSpec as P

HD = 64


rope_base = 500000.0
norm_eps = 1e-05


def sent_together(arrays, axis, dim, along):
    columns = [a.reshape(*a.shape[:along], -1) for a in arrays]
    both = jnp.concatenate(columns, axis=along)
    filled, at, gathered = (lax.all_gather(both, axis, axis=dim, tiled=True), 0, [])
    for a, column in zip(arrays, columns):
        piece = filled[..., at : at + column.shape[along]]
        gathered.append(piece.reshape(*piece.shape[:along], *a.shape[along:]))
        at += column.shape[along]
    return tuple(gathered)


def copy_for_each(array, axis):
    copies = jnp.broadcast_to(array, (lax.axis_size(axis), *array.shape))
    return lax.all_to_all(copies, axis, split_axis=0, concat_axis=0, tiled=True)


def laid_out(blocks, dim):
    blocks = jnp.moveaxis(blocks, 0, dim)
    dims = blocks.shape
    return blocks.reshape(*dims[:dim], dims[dim] * dims[dim + 1], *dims[dim + 2 :])


def gather_directly(array, axis, dim):
    blocks = copy_for_each(array, axis)
    return laid_out(blocks, dim)


def rope_tables(tokens, head_dim):
    position = jnp.arange(tokens, dtype=jnp.float32)
    freq = rope_base ** (-(jnp.arange(head_dim // 2, dtype=jnp.float32) * 2.0) / head_dim)
    angle = position[:, None] * freq[None, :]
    cos_table = jnp.concatenate([jnp.cos(angle), jnp.cos(angle)], axis=-1)
    sin_table = jnp.concatenate([jnp.sin(angle), jnp.sin(angle)], axis=-1)
    return (cos_table, sin_table)


def rotate(tensor, cos_table, sin_table):
    half = tensor.shape[-1] // 2
    turned = jnp.concatenate([-tensor[..., half:], tensor[..., :half]], axis=-1)
    return tensor * cos_table + turned * sin_table


def body(hidden, attn_gain, w_query, w_key, w_value, w_out):
    tokens = hidden.shape[0]
    head_dim = HD
    width_query = w_query.shape[1]
    width_kv = w_key.shape[1]
    kv_count = width_kv // head_dim
    group = width_query // width_kv
    x_float = hidden.astype(jnp.float32)
    inv_rms = lax.rsqrt(jnp.mean(x_float * x_float, axis=-1, keepdims=True) + norm_eps)
    grouped = sent_together((attn_gain, w_query, w_key, w_value), "rep", 0, 1)
    gain_piece, query_piece, key_piece, value_piece = sent_together(
        (grouped[0], grouped[1], grouped[2], grouped[3]), "fsdp", 0, 1
    )
    normed = (x_float * inv_rms * gain_piece.astype(jnp.float32)[None, :]).astype(jnp.bfloat16)
    queries = jnp.dot(normed, query_piece, preferred_element_type=jnp.float32)
    keys_raw = jnp.dot(normed, key_piece, preferred_element_type=jnp.float32)
    values_raw = jnp.dot(normed, value_piece, preferred_element_type=jnp.float32)
    cos_table, sin_table = rope_tables(tokens, head_dim)
    queries = queries.reshape(tokens, kv_count, group, head_dim)
    keys_raw = keys_raw.reshape(tokens, kv_count, head_dim)
    values_bf = values_raw.reshape(tokens, kv_count, head_dim).astype(jnp.bfloat16)
    rope_queries = rotate(queries, cos_table[:, None, None, :], sin_table[:, None, None, :]).astype(
        jnp.bfloat16
    )
    rope_keys = rotate(keys_raw, cos_table[:, None, :], sin_table[:, None, :]).astype(jnp.bfloat16)
    scores = jnp.einsum(
        "qkgd,skd->kgqs", rope_queries, rope_keys, preferred_element_type=jnp.float32
    ) * head_dim ** (-0.5)
    causal = jnp.arange(tokens)[:, None] >= jnp.arange(tokens)[None, :]
    scores = jnp.where(causal[None, None, :, :], scores, -1e30)
    top = jnp.max(scores, axis=-1, keepdims=True)
    expo = jnp.exp(scores - top)
    probs = (expo / jnp.sum(expo, axis=-1, keepdims=True)).astype(jnp.bfloat16)
    context = jnp.einsum("kgqs,skd->qkgd", probs, values_bf, preferred_element_type=jnp.float32)
    context = context.reshape(tokens, width_query).astype(jnp.bfloat16)
    grouped_cols = gather_directly(w_out, "rep", 1)
    branch = jnp.dot(
        context,
        lax.all_gather(grouped_cols, "fsdp", axis=1, tiled=True),
        preferred_element_type=jnp.float32,
    )
    return (x_float + branch).astype(jnp.bfloat16)


def solution(mesh):
    placed = (
        P(("fsdp", "rep"), None),
        P(("fsdp", "rep")),
        P(("fsdp", "rep"), None),
        P(("fsdp", "rep"), None),
        P(("fsdp", "rep"), None),
        P(None, ("fsdp", "rep")),
    )
    return jax.shard_map(
        body, mesh=mesh, in_specs=placed, out_specs=P(("fsdp", "rep"), None), check_vma=False
    )
```

profile of v0, /device:TPU:1, one launch (start us, length us, event | category | flops | bytes accessed | tf_op | source)
XLA Modules:
  0.0 258.1 jit_solution(10988606192208036558)
XLA Ops:
  6.5 0.0 copy-start
  6.5 0.0 all-gather.3.cloned.1.call-start
  6.5 0.8 copy.17
  7.4 0.9 concatenate.17
  8.2 17.1 %all_gather.9 = bf16[64,3073]{1,0:T(8,128)(2,1)} all-gather(bf16[8,3073]{1,0:T(8,128)(2,1)S(1)} %concatenate.17), channel_id=1, replica_groups=mesh['fsdp'=32,'rep'=8] {'rep'}, dimensions={0}, use_global_device_ids=true | all-gather | bytes 442512 | tf_op jit(solution)/shard_map/all_gather | solution.py:16
  25.4 0.0 all-gather.3.cloned.1.call-update
  25.4 0.0 all-gather.5.cloned.1.call-start
  25.4 0.8 broadcast_in_dim.12
  26.2 9.7 %all_to_all.5 = bf16[8,2048,8]{1,2,0:T(8,128)(2,1)} all-to-all(bf16[8,2048,8]{1,2,0:T(8,128)(2,1)S(1)} %broadcast_in_dim.12), channel_id=1, replica_groups=mesh['fsdp'=32,'rep'=8] {'rep'}, dimensions={0} | all-to-all | bytes 524288 | tf_op jit(solution)/shard_map/all_to_all | solution.py:26
  35.9 0.0 all-gather.5.cloned.1.call-update
  36.0 0.2 fusion.33
  36.2 0.0 copy-done
  36.2 0.3 fusion.9
  36.5 110.4 %all-gather.3.cloned.1.call-done = bf16[2048,3073]{1,0:T(8,128)(2,1)} async-done(((bf16[64,3073]{1,0:T(8,128)(2,1)}), bf16[2048,3073]{1,0:T(8,128)(2,1)}) %all-gather.3.cloned.1.call-update) | async-done | bytes 12587024 | tf_op jit(solution)/shard_map/all_gather | solution.py:16
  146.9 1.3 convert_reduce_fusion
  148.2 2.9 %fusion.19 = bf16[256,512]{1,0:T(8,128)(2,1)S(1)} fusion(bf16[2048,3073]{1,0:T(8,128)(2,1)} %all-gather.3.cloned.1.call-done, bf16[256,2048]{1,0:T(8,128)(2,1)S(1)} %copy-done, f32[2048]{0:T(1024)S(1)} %convert_reduce_fusion, f32[256]{0:T(256)S(1)} %add_rsqrt_fusion), kind=kOutput, calls=%fused_computation.26 | convolution fusion | flops 539099136 | bytes 3417088 | tf_op jit(solution)/shard_map/dot_general | solution.py:71
  151.0 0.1 copy.18
  151.2 3.7 %fusion.12 = f32[256,512]{0,1:T(8,128)S(1)} fusion(bf16[2048,3073]{1,0:T(8,128)(2,1)} %all-gather.3.cloned.1.call-done, bf16[256,2048]{1,0:T(8,128)(2,1)S(1)} %copy-done, f32[2048]{0:T(1024)S(1)} %convert_reduce_fusion, f32[256]{0:T(256)S(1)} %add_rsqrt_fusion), kind=kOutput, calls=%fused_computation.18 | convolution fusion | flops 538968064 | bytes 3679232 | tf_op jit(solution)/shard_map/dot_general | solution.py:70
  154.9 10.6 %fusion.1 = f32[256,2048]{0,1:T(8,128)S(1)} fusion(bf16[2048,3073]{1,0:T(8,128)(2,1)} %all-gather.3.cloned.1.call-done, bf16[256,2048]{1,0:T(8,128)(2,1)S(1)} %copy-done, f32[2048]{0:T(1024)S(1)} %convert_reduce_fusion, f32[256]{0:T(256)S(1)} %add_rsqrt_fusion), kind=kOutput, calls=%fused_computation.1 | convolution fusion | flops 2149580800 | bytes 11543552 | tf_op jit(solution)/shard_map/dot_general | solution.py:69
  165.5 0.2 slice_negate_fusion
  165.7 1.5 fusion.22
  167.2 2.3 fusion.40
  169.5 0.9 fusion.18
  170.4 74.1 %all-gather.5.cloned.1.call-done = bf16[2048,2048]{0,1:T(8,128)(2,1)} async-done(((bf16[2048,64]{0,1:T(8,128)(2,1)}), bf16[2048,2048]{0,1:T(8,128)(2,1)}) %all-gather.5.cloned.1.call-update) | async-done | bytes 8388624 | tf_op jit(solution)/shard_map/all_gather | solution.py:93
  244.5 6.7 %fusion.8 = bf16[256,2048]{1,0:T(8,128)(2,1)} fusion(bf16[256,2048]{0,1:T(8,128)(2,1)S(1)} %bitcast.40, bf16[2048,2048]{0,1:T(8,128)(2,1)} %all-gather.5.cloned.1.call-done, bf16[256,2048]{1,0:T(8,128)(2,1)S(1)} %copy-done), kind=kOutput, calls=%fused_computation.14 | convolution fusion | flops 2149056512 | bytes 11534336 | tf_op jit(solution)/shard_map/dot_general | solution.py:91
  (5 shorter events, 0.1 us)
Async XLA Ops:
  6.5 29.7 %copy-start = (bf16[256,2048]{1,0:T(8,128)(2,1)S(1)}, bf16[256,2048]{1,0:T(8,128)(2,1)}, u32[]{:S(2)}) copy-start(bf16[256,2048]{1,0:T(8,128)(2,1)} %param.6) | copy-start | bytes 3145732
  6.5 140.4 %all-gather.3.cloned.1.call-start = ((), (), s32[]{:S(2)}) async-start(), calls=%async_computation.1 | async-start | bytes 13516800 | tf_op jit(solution)/shard_map/all_gather | solution.py:16
  25.4 219.1 %all-gather.5.cloned.1.call-start = ((), (), s32[]{:S(2)}) async-start(), calls=%async_computation.2 | async-start | bytes 8650752 | tf_op jit(solution)/shard_map/all_gather | solution.py:93
Sparse Core Ops, SparseCore 0:
  25.5 121.3 all-gather.2
  149.5 94.9 all-gather.4
where the time goes:
time: 258 us
  waiting for transfers between devices  184 us (71%)
  blocking collectives  26.8 us (10%)
  matrix products  26.3 us (10%)
  between operations  13.5 us (5%)
  other arithmetic  4.28 us (2%)
  local copies, waits for them, and re-layouts  2.62 us (1%)
    all_gather x1, waiting for transfers between devices, sent_together(): lax.all_gather(both, axis, axis=dim, tiled=True)  110 us
    all_gather x1, waiting for transfers between devices, body(): lax.all_gather(grouped_cols, 'fsdp', axis=1, tiled=True)  74.1 us
    all_gather x1, blocking collectives, sent_together(): lax.all_gather(both, axis, axis=dim, tiled=True)  17.1 us
    dot_general x1, matrix products, body(): queries = jnp.dot(normed, query_piece, preferred_element_type=jnp.float32)  10.6 us
    all_to_all x1, blocking collectives, copy_for_each(): return lax.all_to_all(copies, axis, split_axis=0, concat_axis=0, tiled=True)  9.7 us
    dot_general x1, matrix products, body(): jnp.dot(context, lax.all_gather(grouped_cols, 'fsdp', axis=1, tiled=True)...  6.74 us
  transfers between devices with their start and end apart: 2, of which 2 were waited for; matrix products, arithmetic and copies ran while one was open for 10% of the time, Pallas kernels for 0%

commit v1 on v0

v1 whole, which is shorter than its diff:
```python
import math

import jax
import jax.numpy as jnp
import numpy as np
from jax import lax
from jax.experimental import pallas as pl
from jax.experimental.pallas import tpu as pltpu
from jax.sharding import PartitionSpec as P

HD = 64
SEQ = 256
D = 2048
ROPE_BASE = 500000.0
NORM_EPS = 1e-05
MESH = pl.DeviceIdType.MESH

RING = {"x": 4, "y": 4, "z": 8}
ORDER = {"X": "zyx", "Y": "zxy", "Z": "xyz", "G": "xyz"}
LANES = {"X": {"p": 512, "o": 384}, "Y": {"p": 512, "o": 256}, "Z": {"p": 512, "o": 384}, "G": {"g": 32}}
WO_AT = {"X": 0, "Y": 384, "Z": 640}
RATE, LATENCY, ISSUE, BEGIN = 46.6e3, 1.9, 0.1, 4.0


def ring_steps(n, cut):
    for step in range(1, n // 2 + 1):
        for way in (1, -1):
            halves = (0, 1) if way > 0 else (1, 0)
            if step == n // 2:
                yield step, way, halves[:1]
            else:
                yield step, way, halves if cut else (None,)


def list_copies():
    copies, index = [], {}

    def add(key, size, needs):
        index[key] = len(copies)
        copies.append((key, size, [index[n] for n in needs]))

    for name in ORDER:
        first, second, last = ORDER[name]
        lanes = LANES[name]
        got = {(ring, part): [] for ring in range(3) for part in lanes}
        for ring, (axis, blocks) in enumerate(((first, 1), (second, RING[first]), (last, RING[first] * RING[second]))):
            n = RING[axis]
            for part in lanes:
                for step, way, halves in ring_steps(n, ring == 2 and name != "G"):
                    for half in halves:
                        if ring == 0 and name != "G":
                            if step == n // 2 and (part == "p") != (way > 0):
                                continue
                            half = None
                        key = (name, ring, part, step, way, half)
                        if step > 1:
                            before = (name, ring, part, step - 1, way, half)
                            needs = [before if before in index else before[:5] + (None,)]
                        else:
                            needs = got[ring - 1, part] if ring else []
                        size = blocks * lanes[part] * 32 / (1 if half is None else 2)
                        add(key, size, needs)
                        got[ring, part].append(key)
    return copies


def arrange(copies):
    come, free, order = {}, {}, []
    left = set(range(len(copies)))

    def rank(i):
        name, ring, part, step, way, half = copies[i][0]
        return ("gpo".index(part), ring, step, i)

    while left:
        best = None
        ready = {}
        for i in left:
            if all(n in come for n in copies[i][2]):
                key = copies[i][0]
                at = max([come[n] for n in copies[i][2]] + [BEGIN]) + ISSUE
                ready.setdefault((ORDER[key[0]][key[1]], key[4]), []).append((at, i))
        for link in sorted(ready):
            begin = max(free.get(link, 0.0), min(ready[link])[0])
            pick = min((i for at, i in ready[link] if at <= begin + 1e-9), key=rank)
            if best is None or (begin, pick) < best[:2]:
                best = (begin, pick, link)
        begin, pick, link = best
        free[link] = begin + copies[pick][1] / RATE
        come[pick] = free[link] + LATENCY
        left.remove(pick)
        order.append((begin, pick))
    return order, come


COPIES = list_copies()
SENT, COME = arrange(COPIES)
PART = {}
for number, (copy_key, _, _) in enumerate(COPIES):
    PART.setdefault((copy_key[0], copy_key[2]), []).append(number)


def dot(a, b):
    return lax.dot_general(a, b, (((1,), (0,)), ((), ())), preferred_element_type=jnp.float32)


def dot_t(a, b):
    return lax.dot_general(a, b, (((1,), (1,)), ((), ())), preferred_element_type=jnp.float32)


def kernel(
    hidden, gain, wq, wk, wv, wo, cos, sin, out,
    sx, sy, sz, sg, xs, normed, q_all, k_lo, k_hi, v_lo, v_hi, ctx, mine, gone, come,
    local, away, here, sent, got, out_sent, out_got,
):
    f, r = lax.axis_index("fsdp"), lax.axis_index("rep")
    at = {"z": f // 4, "y": f % 4, "x": r // 2}
    core = r % 2
    other = 1 - core
    partner = (f, at["x"] * 2 + other)

    def neighbour(axis, way):
        n = RING[axis]
        place = dict(at)
        place[axis] = (at[axis] + way + n) % n
        return (place["z"] * 4 + place["y"], place["x"] * 2 + core)

    barrier = pltpu.get_barrier_semaphore()
    peers = [partner] + [neighbour(axis, way) for axis in "xyz" for way in (1, -1)]
    for peer in peers:
        pl.semaphore_signal(barrier, inc=1, device_id=peer, device_id_type=MESH)

    buffers = {"X": sx, "Y": sy, "Z": sz, "G": sg}
    rows = pl.ds(pl.multiple_of(core * 8, 8), 8)
    own_rows = pl.ds(pl.multiple_of(core * SEQ, SEQ), SEQ)
    other_rows = pl.ds(pl.multiple_of(other * SEQ, SEQ), SEQ)

    def shares(t):
        def cut(ref, width, start, count):
            return ref.at[:, pl.ds(pl.multiple_of(t * width + start, 128), count)]

        for name, lane, source in (
            ("X", 0, cut(wq, 1024, 0, 512)),
            ("Y", 0, cut(wq, 1024, 512, 512)),
            ("Z", 0, cut(wk, 256, 0, 256)),
            ("Z", 256, cut(wv, 256, 0, 256)),
            ("X", 512, cut(wo, 1024, 0, 384)),
            ("Y", 512, cut(wo, 1024, 384, 256)),
            ("Z", 512, cut(wo, 1024, 640, 384)),
        ):
            a, b, c = (at[axis] for axis in ORDER[name])
            yield source, buffers[name].at[c, b, a, rows, pl.ds(lane, source.shape[1])]
        yield gain, sg.at[at["z"], at["y"], at["x"], core]
        yield hidden, xs.at[own_rows]

    starting = []
    for i, (source, target) in enumerate(shares(core)):
        starting.append(pltpu.make_async_copy(source, target, local.at[i]))
        starting[-1].start()
    tables = []
    pl.semaphore_wait(barrier, len(peers))
    for i, (source, target) in enumerate(shares(other)):
        copy = pltpu.make_async_remote_copy(
            src_ref=source, dst_ref=target, send_sem=away.at[i], recv_sem=here.at[i],
            device_id=partner, device_id_type=MESH,
        )
        copy.start()
        starting.append(copy)
    count = len(starting) // 2
    for copy in starting[: count - 1] + starting[count : 2 * count - 1]:
        copy.wait()

    def halves(n, half):
        return pl.ds(0, n) if half is None else pl.ds(half * (n // 2), n // 2)

    def transfer(i, moved):
        name, ring, part, step, way, half = COPIES[i][0]
        order = ORDER[name]
        a, b, c = (at[axis] for axis in order)
        axis = order[ring]
        n = RING[axis]
        block = (at[axis] - way * (step - 1 + moved) + n) % n
        if name == "G":
            tail = (halves(2, half),) if ring == 0 else ()
        else:
            start = 0 if part == "p" else LANES[name]["p"]
            tail = (slice(None), pl.ds(start, LANES[name][part]))
        if ring == 0:
            where = (c, b, block) + tail
        elif ring == 1:
            where = (c, block, halves(RING[order[0]], half)) + tail
        else:
            where = (block, halves(RING[order[1]], half)) + ((slice(None),) + tail if tail else ())
        ref = buffers[name].at[where]
        return pltpu.make_async_remote_copy(
            src_ref=ref, dst_ref=ref, send_sem=sent.at[i], recv_sem=got.at[i],
            device_id=neighbour(axis, way), device_id_type=MESH,
        )

    arrived = set()

    def await_copy(i):
        if i not in arrived:
            arrived.add(i)
            transfer(i, 1).wait_recv()

    def norm(lo):
        starting_rows = pl.ds(lo, 128)
        x = xs[starting_rows].astype(jnp.float32)
        scale = lax.rsqrt(jnp.mean(x * x, axis=-1, keepdims=True) + NORM_EPS)
        for tile in range(16):
            z, y = tile // 2, tile % 2 * 2
            weight = sg[z, y, 0, 0]
            for k in range(1, 16):
                weight = weight + sg[z, y + k // 8, k // 2 % 4, k % 2]
            lanes = slice(tile * 128, tile * 128 + 128)
            normed[starting_rows, lanes] = (x[:, lanes] * scale * weight).astype(jnp.bfloat16)

    lane = lax.broadcasted_iota(jnp.int32, (SEQ, 128), 1)

    def rope(t):
        turned = jnp.where(lane % 64 < 32, pltpu.roll(t, 96, 1), pltpu.roll(t, 32, 1))
        return t * cos[...] + turned * sin[...]

    def columns(name, lo, n):
        pieces = []
        for z in range(8):
            for y in range(4):
                for x in range(4):
                    place = {"x": x, "y": y, "z": z}
                    a, b, c = (place[axis] for axis in ORDER[name])
                    pieces.append(buffers[name][c, b, a, :, lo : lo + n])
        return jnp.concatenate(pieces, axis=0)

    def project_q(name, lo, start):
        t = dot(normed[...], columns(name, lo, 256))
        for s in range(2):
            for half in range(2):
                piece = rope(t[s * SEQ : s * SEQ + SEQ, half * 128 : half * 128 + 128])
                q_all[s * SEQ : s * SEQ + SEQ, start + half * 128 : start + half * 128 + 128] = (
                    piece * HD**-0.5
                ).astype(jnp.bfloat16)

    def project_kv(lo, turn, low, high):
        t = dot(normed[...], columns("Z", lo, 256))
        for s in range(2):
            for pair in range(2):
                piece = t[s * SEQ : s * SEQ + SEQ, pair * 128 : pair * 128 + 128]
                if turn:
                    piece = rope(piece)
                moved = pltpu.roll(piece, 64, 1)
                zero = jnp.zeros_like(piece)
                here_rows = slice(s * SEQ, s * SEQ + SEQ)
                for odd in range(2):
                    same, swapped = jnp.where(lane < 64, piece, zero), jnp.where(lane < 64, zero, moved)
                    if odd:
                        same, swapped = jnp.where(lane < 64, moved, zero), jnp.where(lane < 64, zero, piece)
                    low[2 * pair + odd, here_rows] = same.astype(jnp.bfloat16)
                    high[2 * pair + odd, here_rows] = swapped.astype(jnp.bfloat16)

    def attend(s, head):
        keys = (k_lo[head, s * SEQ : s * SEQ + SEQ], k_hi[head, s * SEQ : s * SEQ + SEQ])
        values = jnp.concatenate(
            [v_lo[head, s * SEQ : s * SEQ + SEQ], v_hi[head, s * SEQ : s * SEQ + SEQ]], axis=0
        )
        for pair in range(2):
            start = head * 256 + pair * 128
            for block in range(2):
                n = 128 * (block + 1)
                lo = s * SEQ + block * 128
                queries = q_all[lo : lo + 128, start : start + 128]
                probs = []
                for key in keys:
                    scores = dot_t(queries, key[:n])
                    ahead = lax.broadcasted_iota(jnp.int32, (128, n), 1) <= (
                        lax.broadcasted_iota(jnp.int32, (128, n), 0) + block * 128
                    )
                    scores = jnp.where(ahead, scores, -1e30)
                    expo = jnp.exp(scores - jnp.max(scores, axis=-1, keepdims=True))
                    probs.append((expo / jnp.sum(expo, axis=-1, keepdims=True)).astype(jnp.bfloat16))
                mixed = dot(probs[0], values[:n]) + dot(probs[1], values[SEQ : SEQ + n])
                ctx[lo : lo + 128, start : start + 128] = mixed.astype(jnp.bfloat16)

    def await_part(*parts):
        for part in parts:
            for i in PART[part]:
                await_copy(i)

    works = []

    def work(parts, cost, run, *args):
        ready = max(COME[i] for part in parts for i in PART[part])
        works.append((ready, cost, parts, run, args))

    def first_norm():
        starting[count - 1].wait()
        starting[2 * count - 1].wait()

    work([("G", "g")], 0.0, first_norm)
    for lo in range(0, 2 * SEQ, 128):
        work([("G", "g")], 0.6, norm, lo)
    work([("Z", "p")], 0.9, project_kv, 0, True, k_lo, k_hi)
    work([("Z", "p")], 0.9, project_kv, 256, False, v_lo, v_hi)
    for name, start in (("X", 0), ("Y", 512)):
        for lo in (0, 256):
            work([(name, "p")], 0.9, project_q, name, lo, start + lo)
    for name, heads in (("X", (0, 1)), ("Y", (2, 3))):
        for head in heads:
            for s in range(2):
                work([(name, "p"), ("Z", "p")], 1.0, attend, s, head)
    works.sort(key=lambda w: w[0])

    now = 0.0

    def do_work():
        nonlocal now
        ready, cost, parts, run, args = works.pop(0)
        await_part(*parts)
        run(*args)
        now = max(now, ready) + cost

    for begin, i in SENT:
        while works and max(works[0][0], now) + works[0][1] <= begin + 0.3:
            do_work()
        for j in COPIES[i][2]:
            await_copy(j)
        transfer(i, 0).start()
        now = max(now, begin)
    while works:
        do_work()

    for i in range(len(COPIES)):
        await_copy(i)

    def leaving(z):
        return pltpu.make_async_remote_copy(
            src_ref=gone.at[z], dst_ref=come.at[z], send_sem=out_sent.at[z], recv_sem=out_got.at[z],
            device_id=partner, device_id_type=MESH,
        )

    def context_of(chosen):
        return jnp.concatenate([ctx[chosen, :]], axis=0)

    for z in range(8):
        weights = []
        for name in "XYZ":
            lo, n = LANES[name]["p"], LANES[name]["o"]
            pieces = []
            for y in range(4):
                for x in range(4):
                    place = {"x": x, "y": y, "z": z}
                    a, b, c = (place[axis] for axis in ORDER[name])
                    pieces.append(buffers[name][c, b, a, :, lo : lo + n])
            weights.append(jnp.concatenate(pieces, axis=0))
        weights = jnp.concatenate(weights, axis=1)
        gone[z] = dot_t(ctx[other_rows, :], weights)
        leaving(z).start()
        mine[z] = dot_t(ctx[own_rows, :], weights)
    for z in range(8):
        lanes = slice(z * 256, z * 256 + 256)
        leaving(z).wait_recv()
        out[:, lanes] = (xs[own_rows, lanes].astype(jnp.float32) + (mine[z] + come[z])).astype(jnp.bfloat16)
    for z in range(8):
        leaving(z).wait_send()
    for i in range(len(COPIES)):
        transfer(i, 0).wait_send()


def rope_tables():
    position = np.arange(SEQ, dtype=np.float64)
    freq = ROPE_BASE ** (-(np.arange(HD // 2) * 2.0) / HD)
    angle = position[:, None] * freq[None, :]
    cos = np.tile(np.cos(angle), (1, 4))
    sin = np.tile(np.concatenate([-np.sin(angle), np.sin(angle)], axis=1), (1, 2))
    return cos.astype(np.float32), sin.astype(np.float32)


def body(hidden, gain, wq, wk, wv, w_out):
    cos, sin = rope_tables()
    device = lax.axis_index("fsdp") * 8 + lax.axis_index("rep")
    spread = jnp.tile(gain.astype(jnp.float32), 16)
    spread = jnp.where(jnp.arange(128) // 8 == device % 16, spread, 0.0)[None, :]
    vmem = pltpu.VMEM
    bf16, f32 = jnp.bfloat16, jnp.float32
    n = len(COPIES)
    dma = pltpu.SemaphoreType.DMA
    anywhere = pl.BlockSpec(memory_space=pl.ANY)
    inside = pl.BlockSpec(memory_space=pltpu.VMEM)
    return pl.pallas_call(
        kernel,
        out_shape=jax.ShapeDtypeStruct((SEQ, D), bf16),
        in_specs=[anywhere] * 6 + [inside] * 2,
        out_specs=inside,
        scratch_shapes=[
            vmem((4, 4, 8, 16, 896), bf16),
            vmem((4, 4, 8, 16, 768), bf16),
            vmem((8, 4, 4, 16, 896), bf16),
            vmem((8, 4, 4, 2, 1, 128), f32),
            vmem((2 * SEQ, D), bf16),
            vmem((2 * SEQ, D), bf16),
            vmem((2 * SEQ, 1024), bf16),
            vmem((4, 2 * SEQ, 128), bf16),
            vmem((4, 2 * SEQ, 128), bf16),
            vmem((4, 2 * SEQ, 128), bf16),
            vmem((4, 2 * SEQ, 128), bf16),
            vmem((2 * SEQ, 1024), bf16),
            vmem((8, SEQ, 256), f32),
            vmem((8, SEQ, 256), f32),
            vmem((8, SEQ, 256), f32),
            dma((9,)), dma((9,)), dma((9,)), dma((n,)), dma((n,)), dma((8,)), dma((8,)),
        ],
        compiler_params=pltpu.CompilerParams(
            collective_id=0, has_side_effects=True, vmem_limit_bytes=60 * 2**20
        ),
        name="attention_block",
    )(hidden, spread, wq, wk, wv, w_out.T, cos, sin)


def solution(mesh):
    rows = P(("fsdp", "rep"), None)
    placed = (rows, P(("fsdp", "rep")), rows, rows, rows, P(None, ("fsdp", "rep")))
    return jax.shard_map(body, mesh=mesh, in_specs=placed, out_specs=rows, check_vma=False)
```

time: 258 us -> 83.9 us (0.33)
  waiting for transfers between devices: 184 us -> 0 us
  Pallas kernels: 0 us -> 80.1 us
  blocking collectives: 26.8 us -> 0 us
  matrix products: 26.3 us -> 0 us
  between operations: 13.5 us -> 0.01 us
  other arithmetic: 4.28 us -> 0.53 us
    all_gather x2 -> x0, waiting for transfers between devices: 184 us -> none  [the longest x1 110 us: sent_together(): lax.all_gather(both, axis, axis=dim, tiled=True)]
    pallas_call x0 -> x1, Pallas kernels: none -> 80.1 us  [body(): pl.pallas_call(kernel, out_shape=jax.ShapeDtypeStruct((SEQ, D), bf16), in...]
    dot_general x6 -> x0, matrix products: 26.3 us -> none  [the longest x1 10.6 us: body(): queries = jnp.dot(normed, query_piece, preferred_element_type=jnp.float32)]
    all_gather x1 -> x0, blocking collectives: 17.1 us -> none  [sent_together(): lax.all_gather(both, axis, axis=dim, tiled=True)]
    all_to_all x1 -> x0, blocking collectives: 9.7 us -> none  [copy_for_each(): return lax.all_to_all(copies, axis, split_axis=0, concat_axis=0, tiled=True)]
    unnamed x2 -> x3, local copies, waits for them, and re-layouts: 0.01 us -> 2.96 us
  transfers between devices with their start and end apart: 2 -> 0, of which waited for: 2 -> 0; matrix products, arithmetic and copies ran while one was open for 10% -> 0% of each run, Pallas kernels for 0% -> 0%
where the time goes in v1:
time: 83.9 us; the launch traced here: 83.7 us
  Pallas kernels  80.1 us (95%)
  local copies, waits for them, and re-layouts  3.05 us (4%)
    pallas_call x1, Pallas kernels, body(): pl.pallas_call(kernel, out_shape=jax.ShapeDtypeStruct((SEQ, D), bf16), in...  80.1 us
    unnamed x3, local copies, waits for them, and re-layouts  2.96 us

profile of v1, /device:TPU:1, one launch (start us, length us, event | category | flops | bytes accessed | tf_op | source)
XLA Modules:
  0.0 83.7 jit_solution(13301241671122223486)
XLA Ops:
  0.0 0.0 copy-start
  0.0 0.7 copy-done
  0.7 0.1 tile.10
  0.7 0.5 compare_select_fusion.gain
  1.3 80.1 %attention_block.1 = bf16[256,2048]{1,0:T(8,128)(2,1)} custom-call(bf16[256,2048]{1,0:T(8,128)(2,1)} %hidden.1, f32[1,128]{1,0:T(1,128)} %compare_select_fusion.gain, bf16[8,2048]{1,0:T(8,128)(2,1)} %wq.1, bf16[8,512]{1,0:T(8,128)(2,1)} %wk.1, bf16[8,512]{1,0:T(8,128)(2,1)} %wv.1, bf16[8,2048]{1,0:T(8,128)(2,1)} %bitcast.1, f32[256,128]{1,0:T(8,128)} %constant.46.clone.cos, ...), custom_call_target="tpu_custom_call" | custom-call | tf_op jit(solution)/shard_map/attention_block/pallas_call | solution.py:389
  81.4 2.3 %copy.10 = bf16[256,2048]{1,0:T(8,128)(2,1)} copy(bf16[256,2048]{1,0:T(8,128)(2,1)} %attention_block.1) | data formatting | bytes 2097152
  (1 shorter events, 0.0 us)
Async XLA Ops:
  0.0 0.7 copy-start

commit v2 on v1

v2 whole, which is shorter than its diff:
```python
import math

import jax
import jax.numpy as jnp
import numpy as np
from jax import lax
from jax.experimental import pallas as pl
from jax.experimental.pallas import tpu as pltpu
from jax.sharding import PartitionSpec as P

HD = 64
SEQ = 256
D = 2048
ROPE_BASE = 500000.0
NORM_EPS = 1e-05
MESH = pl.DeviceIdType.MESH

RING = {"x": 4, "y": 4, "z": 8}
ORDER = {"X": "zyx", "Y": "zxy", "Z": "yxz", "G": "xyz"}
LANES = {"X": {"p": 512, "o": 384}, "Y": {"p": 512, "o": 256}, "Z": {"p": 512, "o": 384}, "G": {"g": 32}}
GROUPS = {8: ((0, 3), (3, 2), (5, 3)), 4: ((0, 1), (1, 2), (3, 1))}
RATE, LATENCY, ISSUE, BEGIN = 46.6e3, 2.2, 0.1, 4.0


def slot(n, step, way):
    return n - 1 if step == n // 2 else 2 * step - (way < 0 and step > 0)


def list_copies():
    copies, index = [], {}

    def go_round(prefix, axis, size, first, cut):
        n, made = RING[axis], []
        for step in range(1, n // 2 + 1):
            for way in (1, -1):
                halves = (0, 1) if way > 0 else (1, 0)
                for half in halves[:1] if step == n // 2 else halves if cut else (None,):
                    key = prefix + (step, way, half)
                    before = prefix + (step - 1, way, half)
                    if before not in index:
                        before = prefix + (step - 1, way, None)
                    needs = first if step == 1 else [before]
                    index[key] = len(copies)
                    copies.append((key, size / (1 if half is None else 2), [index[k] for k in needs]))
                    made.append(key)
        return made

    for name, (first, second, last) in ORDER.items():
        n = RING[first]
        for part, lanes in LANES[name].items():
            made = go_round((part, name, 0, (0, n)), first, lanes * 32, [], False)
            for group in GROUPS[n] if part == "p" else ((0, n),):
                needs = [k for k in made if group[0] <= slot(n, k[4], k[5]) < sum(group)]
                size = lanes * 32 * group[1]
                passed = go_round((part, name, 1, group), second, size, needs, False)
                go_round((part, name, 2, group), last, size * RING[second], passed, part == "o")
    return copies


def arrange(copies):
    come, free, order = {}, {}, []
    left = set(range(len(copies)))

    def rank(i):
        part, name, ring, group, step, way, half = copies[i][0]
        return (part != "g", ring == 2 and part == "o", ring, -step, i)

    while left:
        best = None
        ready = {}
        for i in left:
            if all(n in come for n in copies[i][2]):
                key = copies[i][0]
                at = max([come[n] for n in copies[i][2]] + [BEGIN]) + ISSUE
                ready.setdefault((ORDER[key[1]][key[2]], key[5]), []).append((at, i))
        for link in sorted(ready):
            begin = max(free.get(link, 0.0), min(ready[link])[0])
            pick = min((i for at, i in ready[link] if at <= begin + 1e-9), key=rank)
            if best is None or (begin, pick) < best[:2]:
                best = (begin, pick, link)
        begin, pick, link = best
        free[link] = begin + copies[pick][1] / RATE
        come[pick] = free[link] + LATENCY
        left.remove(pick)
        order.append((begin, pick))
    return order, come


COPIES = list_copies()
SENT, COME = arrange(COPIES)
PART = {}
for number, (copy_key, _, _) in enumerate(COPIES):
    PART.setdefault((copy_key[1], copy_key[0]), []).append(number)
FAR = [(0, 0), (1, 1), (1, -1), (2, 1), (2, -1), (3, 1), (3, -1), (4, 1)]
LAST = {}
for number, (copy_key, _, _) in enumerate(COPIES):
    if copy_key[:3] == ("o", "Z", 2):
        LAST.setdefault((copy_key[4], 1 if copy_key[4] == 4 else copy_key[5]), []).append(number)


def dot(a, b):
    return lax.dot_general(a, b, (((1,), (0,)), ((), ())), preferred_element_type=jnp.float32)


def dot_t(a, b):
    return lax.dot_general(a, b, (((1,), (1,)), ((), ())), preferred_element_type=jnp.float32)


def kernel(
    hidden, gain, wq, wk, wv, wo, cos_in, sin_in, out,
    px, py, pz, ox, oy, oz, sg, xs, cos, sin, normed, q_all, k_lo, k_hi, v_lo, v_hi,
    score, prob, ctx, acc, mine, gone, come,
    local, away, here, sent, got, out_sent, out_got,
):
    f, r = lax.axis_index("fsdp"), lax.axis_index("rep")
    at = {"z": f // 4, "y": f % 4, "x": r // 2}
    core = r % 2
    other = 1 - core
    partner = (f, at["x"] * 2 + other)

    def neighbour(axis, way):
        n = RING[axis]
        place = dict(at)
        place[axis] = (at[axis] + way + n) % n
        return (place["z"] * 4 + place["y"], place["x"] * 2 + core)

    barrier = pltpu.get_barrier_semaphore()
    peers = [partner] + [neighbour(axis, way) for axis in "xyz" for way in (1, -1)]
    for peer in peers:
        pl.semaphore_signal(barrier, inc=1, device_id=peer, device_id_type=MESH)

    buffers = {"Xp": px, "Yp": py, "Zp": pz, "Xo": ox, "Yo": oy, "Zo": oz, "Gg": sg}
    rows = pl.ds(pl.multiple_of(core * 8, 8), 8)
    own_rows = pl.ds(pl.multiple_of(core * SEQ, SEQ), SEQ)
    other_rows = pl.ds(pl.multiple_of(other * SEQ, SEQ), SEQ)

    def shares(t):
        def cut(ref, width, start, count):
            return ref.at[:, pl.ds(pl.multiple_of(t * width + start, 128), count)]

        for name, lane, source in (
            ("Xp", 0, cut(wq, 1024, 0, 512)),
            ("Yp", 0, cut(wq, 1024, 512, 512)),
            ("Zp", 0, cut(wk, 256, 0, 256)),
            ("Zp", 256, cut(wv, 256, 0, 256)),
            ("Xo", 0, cut(wo, 1024, 0, 384)),
            ("Yo", 0, cut(wo, 1024, 384, 256)),
            ("Zo", 0, cut(wo, 1024, 640, 384)),
        ):
            _, b, c = (at[axis] for axis in ORDER[name[0]])
            yield source, buffers[name].at[c, b, 0, rows, pl.ds(lane, source.shape[1])]
        yield gain, sg.at[at["z"], at["y"], 0, core]
        yield hidden, xs.at[own_rows]

    starting = []
    for i, (source, target) in enumerate(shares(core)):
        starting.append(pltpu.make_async_copy(source, target, local.at[i]))
        starting[-1].start()
    tables = [
        pltpu.make_async_copy(cos_in, cos, local.at[9]),
        pltpu.make_async_copy(sin_in, sin, local.at[10]),
    ]
    for copy in tables:
        copy.start()
    pl.semaphore_wait(barrier, len(peers))
    for i, (source, target) in enumerate(shares(other)):
        copy = pltpu.make_async_remote_copy(
            src_ref=source, dst_ref=target, send_sem=away.at[i], recv_sem=here.at[i],
            device_id=partner, device_id_type=MESH,
        )
        copy.start()
        starting.append(copy)
    count = len(starting) // 2
    for copy in starting[: count - 1] + starting[count : 2 * count - 1]:
        copy.wait()

    def halves(n, half):
        return pl.ds(0, n) if half is None else pl.ds(half * (n // 2), n // 2)

    def lane_half(n, half):
        first = (n // 128 + 1) // 2 * 128
        return pl.ds(0, n) if half is None else pl.ds(0, first) if half == 0 else pl.ds(first, n - first)

    def transfer(i):
        part, name, ring, group, step, way, half = COPIES[i][0]
        a, b, c = (at[axis] for axis in ORDER[name])
        axis = ORDER[name][ring]
        n = RING[axis]
        buffer = buffers[name + part]
        lanes = LANES[name][part]
        block = (at[axis] - way * (step - 1) + n) % n
        source = target = None
        if ring == 0:
            tail = (halves(2, half),) if part == "g" else (slice(None), lane_half(lanes, half))
            source = buffer.at[(c, b, slot(n, step - 1, way)) + tail]
            target = buffer.at[(c, b, slot(n, step, way)) + tail]
        elif ring == 1:
            slots = pl.ds(*group)
            if part == "g":
                source = target = buffer.at[c, block, halves(group[1], half)]
            else:
                source = target = buffer.at[c, block, slots, :, lane_half(lanes, half)]
        else:
            slots = pl.ds(*group)
            source = target = buffer.at[block, halves(RING[ORDER[name][1]], half), slots]
        return pltpu.make_async_remote_copy(
            src_ref=source, dst_ref=target, send_sem=sent.at[i], recv_sem=got.at[i],
            device_id=neighbour(axis, way), device_id_type=MESH,
        )

    def incoming(i):
        part, name, ring, group, step, way, half = COPIES[i][0]
        if ring == 0:
            return transfer(i)
        a, b, c = (at[axis] for axis in ORDER[name])
        axis = ORDER[name][ring]
        n = RING[axis]
        buffer = buffers[name + part]
        lanes = LANES[name][part]
        block = (at[axis] - way * step + n) % n
        if ring == 1 and part == "g":
            target = buffer.at[c, block, halves(group[1], half)]
        elif ring == 1:
            target = buffer.at[c, block, pl.ds(*group), :, lane_half(lanes, half)]
        else:
            target = buffer.at[block, halves(RING[ORDER[name][1]], half), pl.ds(*group)]
        return pltpu.make_async_remote_copy(
            src_ref=target, dst_ref=target, send_sem=sent.at[i], recv_sem=got.at[i],
            device_id=neighbour(axis, way), device_id_type=MESH,
        )

    arrived = set()

    def await_copy(i):
        if i not in arrived:
            arrived.add(i)
            incoming(i).wait_recv()

    def slots_of(axis):
        n = RING[axis]
        found = []
        for place in range(n):
            d = (place - at[axis] + n) % n
            found.append(jnp.where(d == 0, 0, jnp.where(d <= n // 2, 2 * d - 1, 2 * (n - d))))
        return found

    place_slots = {axis: slots_of(axis) for axis in "yz"}

    def norm(lo):
        chosen = pl.ds(lo, 128)
        x = xs[chosen].astype(jnp.float32)
        scale = lax.rsqrt(jnp.mean(x * x, axis=-1, keepdims=True) + NORM_EPS)
        for tile in range(16):
            z, y = tile // 2, tile % 2 * 2
            weight = sg[z, y, 0, 0]
            for k in range(1, 16):
                weight = weight + sg[z, y + k // 8, k // 2 % 4, k % 2]
            lanes = slice(tile * 128, tile * 128 + 128)
            normed[chosen, lanes] = (x[:, lanes] * scale * weight).astype(jnp.bfloat16)

    lane = lax.broadcasted_iota(jnp.int32, (SEQ, 128), 1)

    def rope(t):
        turned = jnp.where(lane % 64 < 32, pltpu.roll(t, 96, 1), pltpu.roll(t, 32, 1))
        return t * cos[...] + turned * sin[...]

    def features(name, z, lo, n):
        first, second, last = ORDER[name[0]]
        pieces = []
        for y in range(4):
            for x in range(4):
                place = {"x": x, "y": y, "z": z}
                pieces.append(
                    buffers[name][place[last], place[second], place_slots[first][place[first]], :, lo : lo + n]
                )
        return pieces

    def columns(name, lo, n):
        return jnp.concatenate([piece for z in range(8) for piece in features(name, z, lo, n)], axis=0)

    def project_q(name, lo, start):
        t = dot(normed[...], columns(name, lo, 256))
        for s in range(2):
            for half in range(2):
                piece = rope(t[s * SEQ : s * SEQ + SEQ, half * 128 : half * 128 + 128])
                q_all[s * SEQ : s * SEQ + SEQ, start + half * 128 : start + half * 128 + 128] = (
                    piece * HD**-0.5
                ).astype(jnp.bfloat16)

    def project_kv(lo, turn, low, high):
        t = dot(normed[...], columns("Zp", lo, 256))
        for s in range(2):
            for pair in range(2):
                piece = t[s * SEQ : s * SEQ + SEQ, pair * 128 : pair * 128 + 128]
                if turn:
                    piece = rope(piece)
                moved = pltpu.roll(piece, 64, 1)
                zero = jnp.zeros_like(piece)
                here_rows = slice(s * SEQ, s * SEQ + SEQ)
                for odd in range(2):
                    same, swapped = jnp.where(lane < 64, piece, zero), jnp.where(lane < 64, zero, moved)
                    if odd:
                        same, swapped = jnp.where(lane < 64, moved, zero), jnp.where(lane < 64, zero, piece)
                    low[2 * pair + odd, here_rows] = same.astype(jnp.bfloat16)
                    high[2 * pair + odd, here_rows] = swapped.astype(jnp.bfloat16)

    def attend(s, head):
        here_rows = slice(s * SEQ, s * SEQ + SEQ)
        keys = (k_lo[head, here_rows], k_hi[head, here_rows])
        values = jnp.concatenate([v_lo[head, here_rows], v_hi[head, here_rows]], axis=0)
        for pair in range(2):
            start = head * 256 + pair * 128
            for odd in range(2):
                score[2 * pair + odd] = dot_t(q_all[here_rows, start : start + 128], keys[odd])
        for unit in range(4):
            for block in range(4):
                n = 128 * (block // 2 + 1)
                chosen = slice(block * 64, block * 64 + 64)
                t = score[unit, chosen, :n]
                seen = lax.broadcasted_iota(jnp.int32, (64, n), 1) <= (
                    lax.broadcasted_iota(jnp.int32, (64, n), 0) + block * 64
                )
                t = jnp.where(seen, t, -1e30)
                expo = jnp.exp(t - jnp.max(t, axis=-1, keepdims=True))
                share = 1.0 / jnp.sum(expo, axis=-1, keepdims=True)
                prob[unit // 2, chosen, unit % 2 * SEQ : unit % 2 * SEQ + n] = (expo * share).astype(jnp.bfloat16)
        for pair in range(2):
            start = head * 256 + pair * 128
            ctx[here_rows, start : start + 128] = dot(prob[pair], values).astype(jnp.bfloat16)

    def mix_first(z):
        weights = jnp.concatenate(
            [
                jnp.concatenate(features("Xo", z, 0, 384), axis=0),
                jnp.concatenate(features("Yo", z, 0, 256), axis=0),
            ],
            axis=1,
        )
        acc[z] = dot_t(ctx[:, :640], weights)

    def chunk_of(k):
        step, way = FAR[k]
        return (at["z"] - way * step + 8) % 8

    def leaving(k):
        return pltpu.make_async_remote_copy(
            src_ref=gone.at[k], dst_ref=come.at[k], send_sem=out_sent.at[k], recv_sem=out_got.at[k],
            device_id=partner, device_id_type=MESH,
        )

    def mix_last(k):
        z = chunk_of(k)
        weights = jnp.concatenate(features("Zo", z, 0, 384), axis=0)
        gone[k] = acc[z, other_rows] + dot_t(ctx[other_rows, 640:], weights)
        mine[k] = acc[z, own_rows] + dot_t(ctx[own_rows, 640:], weights)
        leaving(k).start()

    works = []

    def work(parts, cost, run, *args, needs=()):
        needs = list(needs) + [i for part in parts for i in PART[part]]
        works.append((max(COME[i] for i in needs), cost, needs, run, args))

    def prepare():
        starting[count - 1].wait()
        starting[2 * count - 1].wait()
        for copy in tables:
            copy.wait()
        for pair in range(2):
            for odd in range(2):
                prob[pair, :128, odd * SEQ + 128 : odd * SEQ + SEQ] = jnp.zeros((128, 128), jnp.bfloat16)

    work([("G", "g")], 0.0, prepare)
    for lo in range(0, 2 * SEQ, 128):
        work([("G", "g")], 0.2, norm, lo)
    work([("Z", "p")], 0.8, project_kv, 0, True, k_lo, k_hi)
    work([("Z", "p")], 0.8, project_kv, 256, False, v_lo, v_hi)
    for name, start in (("X", 0), ("Y", 512)):
        for lo in (0, 256):
            work([(name, "p")], 0.8, project_q, name + "p", lo, start + lo)
    works[5:] = sorted(works[5:], key=lambda w: w[0])
    for name, heads in (("X", (0, 1)), ("Y", (2, 3))):
        for head in heads:
            for s in range(2):
                work([(name, "p"), ("Z", "p")], 1.0, attend, s, head)
    for z in range(8):
        work([("X", "o"), ("Y", "o")], 0.4, mix_first, z)
    for k in range(8):
        work([], 0.3, mix_last, k, needs=LAST[FAR[k]] if k else [i for i in PART["Z", "o"] if COPIES[i][0][2] < 2])

    now = 0.0

    def do_work():
        nonlocal now
        ready, cost, needs, run, args = works.pop(0)
        for i in needs:
            await_copy(i)
        run(*args)
        now = max(now, ready) + cost

    for begin, i in SENT:
        while works and max(works[0][0], now) + works[0][1] <= begin + 0.3:
            do_work()
        for j in COPIES[i][2]:
            await_copy(j)
        transfer(i).start()
        now = max(now, begin)
    while works:
        do_work()
    for i in range(len(COPIES)):
        await_copy(i)

    for k in range(8):
        lanes = pl.ds(pl.multiple_of(chunk_of(k) * 256, 256), 256)
        leaving(k).wait_recv()
        out[:, lanes] = (xs[own_rows, lanes].astype(jnp.float32) + (mine[k] + come[k])).astype(jnp.bfloat16)
    for k in range(8):
        leaving(k).wait_send()
    for i in range(len(COPIES)):
        transfer(i).wait_send()


def rope_tables():
    position = np.arange(SEQ, dtype=np.float64)
    freq = ROPE_BASE ** (-(np.arange(HD // 2) * 2.0) / HD)
    angle = position[:, None] * freq[None, :]
    cos = np.tile(np.cos(angle), (1, 4))
    sin = np.tile(np.concatenate([-np.sin(angle), np.sin(angle)], axis=1), (1, 2))
    return cos.astype(np.float32), sin.astype(np.float32)


def body(hidden, gain, wq, wk, wv, w_out):
    cos, sin = rope_tables()
    device = lax.axis_index("fsdp") * 8 + lax.axis_index("rep")
    spread = jnp.tile(gain.astype(jnp.float32), 16)
    spread = jnp.where(jnp.arange(128) // 8 == device % 16, spread, 0.0)[None, :]
    vmem = pltpu.VMEM
    bf16, f32 = jnp.bfloat16, jnp.float32
    n = len(COPIES)
    dma = pltpu.SemaphoreType.DMA
    anywhere = pl.BlockSpec(memory_space=pl.ANY)
    inside = pl.BlockSpec(memory_space=pltpu.VMEM)
    return pl.pallas_call(
        kernel,
        out_shape=jax.ShapeDtypeStruct((SEQ, D), bf16),
        in_specs=[anywhere] * 8,
        out_specs=inside,
        scratch_shapes=[
            vmem((4, 4, 8, 16, 512), bf16),
            vmem((4, 4, 8, 16, 512), bf16),
            vmem((8, 4, 4, 16, 512), bf16),
            vmem((4, 4, 8, 16, 384), bf16),
            vmem((4, 4, 8, 16, 256), bf16),
            vmem((8, 4, 4, 16, 384), bf16),
            vmem((8, 4, 4, 2, 1, 128), f32),
            vmem((2 * SEQ, D), bf16),
            vmem((SEQ, 128), f32),
            vmem((SEQ, 128), f32),
            vmem((2 * SEQ, D), bf16),
            vmem((2 * SEQ, 1024), bf16),
            vmem((4, 2 * SEQ, 128), bf16),
            vmem((4, 2 * SEQ, 128), bf16),
            vmem((4, 2 * SEQ, 128), bf16),
            vmem((4, 2 * SEQ, 128), bf16),
            vmem((4, SEQ, SEQ), f32),
            vmem((2, SEQ, 2 * SEQ), bf16),
            vmem((2 * SEQ, 1024), bf16),
            vmem((8, 2 * SEQ, 256), f32),
            vmem((8, SEQ, 256), f32),
            vmem((8, SEQ, 256), f32),
            vmem((8, SEQ, 256), f32),
            dma((11,)), dma((9,)), dma((9,)), dma((n,)), dma((n,)), dma((8,)), dma((8,)),
        ],
        compiler_params=pltpu.CompilerParams(
            collective_id=0, has_side_effects=True, vmem_limit_bytes=60 * 2**20
        ),
        name="attention_block",
    )(hidden, spread, wq, wk, wv, w_out.T, cos, sin)


def solution(mesh):
    rows = P(("fsdp", "rep"), None)
    placed = (rows, P(("fsdp", "rep")), rows, rows, rows, P(None, ("fsdp", "rep")))
    return jax.shard_map(body, mesh=mesh, in_specs=placed, out_specs=rows, check_vma=False)
```

time: 83.9 us -> 75.3 us (0.90)
  Pallas kernels: 80.1 us -> 71.6 us
    pallas_call x1, Pallas kernels: 80.1 us -> 71.6 us  [body(): pl.pallas_call(kernel, out_shape=jax.ShapeDtypeStruct((SEQ, D), bf16), in...]
where the time goes in v2:
time: 75.3 us; the launch traced here: 75.1 us
  Pallas kernels  71.6 us (95%)
  local copies, waits for them, and re-layouts  3.05 us (4%)
    pallas_call x1, Pallas kernels, body(): pl.pallas_call(kernel, out_shape=jax.ShapeDtypeStruct((SEQ, D), bf16), in...  71.6 us
    unnamed x3, local copies, waits for them, and re-layouts  2.96 us

profile of v2, /device:TPU:1, one launch (start us, length us, event | category | flops | bytes accessed | tf_op | source)
XLA Modules:
  0.0 75.1 jit_solution(1688311451042120463)
XLA Ops:
  0.0 0.0 copy-start
  0.0 0.7 copy-done
  0.7 0.1 tile.10
  0.7 0.5 compare_select_fusion.gain
  1.3 71.6 %attention_block.1 = bf16[256,2048]{1,0:T(8,128)(2,1)} custom-call(bf16[256,2048]{1,0:T(8,128)(2,1)} %hidden.1, f32[1,128]{1,0:T(1,128)} %compare_select_fusion.gain, bf16[8,2048]{1,0:T(8,128)(2,1)} %wq.1, bf16[8,512]{1,0:T(8,128)(2,1)} %wk.1, bf16[8,512]{1,0:T(8,128)(2,1)} %wv.1, bf16[8,2048]{1,0:T(8,128)(2,1)} %bitcast.1, ...), custom_call_target="tpu_custom_call" | custom-call | tf_op jit(solution)/shard_map/attention_block/pallas_call | solution.py:443
  72.8 2.3 %copy.10 = bf16[256,2048]{1,0:T(8,128)(2,1)} copy(bf16[256,2048]{1,0:T(8,128)(2,1)} %attention_block.1) | data formatting | bytes 2097152
  (1 shorter events, 0.0 us)
Async XLA Ops:
  0.0 0.7 copy-start

commit v3 on v2

--- a/solution.py
+++ b/solution.py
@@ -18,7 +18,8 @@
 RING = {"x": 4, "y": 4, "z": 8}
 ORDER = {"X": "zyx", "Y": "zxy", "Z": "yxz", "G": "xyz"}
 LANES = {"X": {"p": 512, "o": 384}, "Y": {"p": 512, "o": 256}, "Z": {"p": 512, "o": 384}, "G": {"g": 32}}
-GROUPS = {8: ((0, 3), (3, 2), (5, 3)), 4: ((0, 1), (1, 2), (3, 1))}
+GROUPS = {8: ((0, 1), (1, 2), (3, 2), (5, 3)), 4: ((0, 1), (1, 2), (3, 1))}
+RANK = {"g": (-1, -1, -1), "p": (0, 1, 3), "o": (1, 3, 7)}
 RATE, LATENCY, ISSUE, BEGIN = 46.6e3, 2.2, 0.1, 4.0
 
 
@@ -63,7 +64,7 @@
 
     def rank(i):
         part, name, ring, group, step, way, half = copies[i][0]
-        return (part != "g", ring == 2 and part == "o", ring, -step, i)
+        return (RANK[part][ring] - 0.2 * step, i)
 
     while left:
         best = None
@@ -110,7 +111,7 @@
     hidden, gain, wq, wk, wv, wo, cos_in, sin_in, out,
     px, py, pz, ox, oy, oz, sg, xs, cos, sin, normed, q_all, k_lo, k_hi, v_lo, v_hi,
     score, prob, ctx, acc, mine, gone, come,
-    local, away, here, sent, got, out_sent, out_got,
+    stage, local, staged, away, here, sent, got, out_sent, out_got,
 ):
     f, r = lax.axis_index("fsdp"), lax.axis_index("rep")
     at = {"z": f // 4, "y": f % 4, "x": r // 2}
@@ -156,6 +157,12 @@
     for i, (source, target) in enumerate(shares(core)):
         starting.append(pltpu.make_async_copy(source, target, local.at[i]))
         starting[-1].start()
+    widths = [source.shape[1] for source, _ in list(shares(other))[:7]]
+    kept = [stage.at[:, pl.ds(sum(widths[:i]), width)] for i, width in enumerate(widths)]
+    staging = []
+    for i, (source, _) in enumerate(list(shares(other))[:7]):
+        staging.append(pltpu.make_async_copy(source, kept[i], staged.at[i]))
+        staging[-1].start()
     tables = [
         pltpu.make_async_copy(cos_in, cos, local.at[9]),
         pltpu.make_async_copy(sin_in, sin, local.at[10]),
@@ -164,6 +171,9 @@
         copy.start()
     pl.semaphore_wait(barrier, len(peers))
     for i, (source, target) in enumerate(shares(other)):
+        if i < 7:
+            staging[i].wait()
+            source = kept[i]
         copy = pltpu.make_async_remote_copy(
             src_ref=source, dst_ref=target, send_sem=away.at[i], recv_sem=here.at[i],
             device_id=partner, device_id_type=MESH,
@@ -208,25 +218,22 @@
             device_id=neighbour(axis, way), device_id_type=MESH,
         )
 
-    def incoming(i):
+    def waiting(i):
         part, name, ring, group, step, way, half = COPIES[i][0]
-        if ring == 0:
-            return transfer(i)
-        a, b, c = (at[axis] for axis in ORDER[name])
-        axis = ORDER[name][ring]
-        n = RING[axis]
         buffer = buffers[name + part]
         lanes = LANES[name][part]
-        block = (at[axis] - way * step + n) % n
-        if ring == 1 and part == "g":
-            target = buffer.at[c, block, halves(group[1], half)]
+        if ring == 0:
+            tail = (halves(2, half),) if part == "g" else (slice(None), lane_half(lanes, half))
+            ref = buffer.at[(0, 0, 0) + tail]
+        elif ring == 1 and part == "g":
+            ref = buffer.at[0, 0, halves(group[1], half)]
         elif ring == 1:
-            target = buffer.at[c, block, pl.ds(*group), :, lane_half(lanes, half)]
+            ref = buffer.at[0, 0, pl.ds(*group), :, lane_half(lanes, half)]
         else:
-            target = buffer.at[block, halves(RING[ORDER[name][1]], half), pl.ds(*group)]
+            ref = buffer.at[0, halves(RING[ORDER[name][1]], half), pl.ds(*group)]
         return pltpu.make_async_remote_copy(
-            src_ref=target, dst_ref=target, send_sem=sent.at[i], recv_sem=got.at[i],
-            device_id=neighbour(axis, way), device_id_type=MESH,
+            src_ref=ref, dst_ref=ref, send_sem=sent.at[i], recv_sem=got.at[i],
+            device_id=partner, device_id_type=MESH,
         )
 
     arrived = set()
@@ -234,7 +241,7 @@
     def await_copy(i):
         if i not in arrived:
             arrived.add(i)
-            incoming(i).wait_recv()
+            waiting(i).wait_recv()
 
     def slots_of(axis):
         n = RING[axis]
@@ -311,22 +318,27 @@
         for pair in range(2):
             start = head * 256 + pair * 128
             for odd in range(2):
-                score[2 * pair + odd] = dot_t(q_all[here_rows, start : start + 128], keys[odd])
+                score[4 * s + 2 * pair + odd] = dot_t(q_all[here_rows, start : start + 128], keys[odd])
         for unit in range(4):
             for block in range(4):
                 n = 128 * (block // 2 + 1)
                 chosen = slice(block * 64, block * 64 + 64)
-                t = score[unit, chosen, :n]
-                seen = lax.broadcasted_iota(jnp.int32, (64, n), 1) <= (
-                    lax.broadcasted_iota(jnp.int32, (64, n), 0) + block * 64
+                seen = lax.broadcasted_iota(jnp.int32, (64, 128), 1) <= (
+                    lax.broadcasted_iota(jnp.int32, (64, 128), 0) + block % 2 * 64
                 )
-                t = jnp.where(seen, t, -1e30)
+                t = jnp.where(seen, score[4 * s + unit, chosen, n - 128 : n], -1e30)
+                if n > 128:
+                    t = jnp.concatenate([score[4 * s + unit, chosen, :128], t], axis=1)
                 expo = jnp.exp(t - jnp.max(t, axis=-1, keepdims=True))
-                share = 1.0 / jnp.sum(expo, axis=-1, keepdims=True)
-                prob[unit // 2, chosen, unit % 2 * SEQ : unit % 2 * SEQ + n] = (expo * share).astype(jnp.bfloat16)
+                share = pl.reciprocal(jnp.sum(expo, axis=-1, keepdims=True), approx=False)
+                prob[2 * s + unit // 2, chosen, unit % 2 * SEQ : unit % 2 * SEQ + n] = (expo * share).astype(jnp.bfloat16)
         for pair in range(2):
             start = head * 256 + pair * 128
-            ctx[here_rows, start : start + 128] = dot(prob[pair], values).astype(jnp.bfloat16)
+            ctx[here_rows, start : start + 128] = dot(prob[2 * s + pair], values).astype(jnp.bfloat16)
+
+    def attend_both(head):
+        for s in range(2):
+            attend(s, head)
 
     def mix_first(z):
         weights = jnp.concatenate(
@@ -359,14 +371,14 @@
 
     def work(parts, cost, run, *args, needs=()):
         needs = list(needs) + [i for part in parts for i in PART[part]]
-        works.append((max(COME[i] for i in needs), cost, needs, run, args))
+        works.append((max(COME[i] for i in needs), cost * 0.6, needs, run, args))
 
     def prepare():
         starting[count - 1].wait()
         starting[2 * count - 1].wait()
         for copy in tables:
             copy.wait()
-        for pair in range(2):
+        for pair in range(4):
             for odd in range(2):
                 prob[pair, :128, odd * SEQ + 128 : odd * SEQ + SEQ] = jnp.zeros((128, 128), jnp.bfloat16)
 
@@ -381,14 +393,14 @@
     works[5:] = sorted(works[5:], key=lambda w: w[0])
     for name, heads in (("X", (0, 1)), ("Y", (2, 3))):
         for head in heads:
-            for s in range(2):
-                work([(name, "p"), ("Z", "p")], 1.0, attend, s, head)
+            work([(name, "p"), ("Z", "p")], 1.7, attend_both, head)
     for z in range(8):
         work([("X", "o"), ("Y", "o")], 0.4, mix_first, z)
     for k in range(8):
         work([], 0.3, mix_last, k, needs=LAST[FAR[k]] if k else [i for i in PART["Z", "o"] if COPIES[i][0][2] < 2])
 
     now = 0.0
+    sending = []
 
     def do_work():
         nonlocal now
@@ -405,6 +417,9 @@
             await_copy(j)
         transfer(i).start()
         now = max(now, begin)
+        sending.append((begin + COPIES[i][1] / RATE + 3.0, i))
+        while sending[0][0] < begin:
+            waiting(sending.pop(0)[1]).wait_send()
     while works:
         do_work()
     for i in range(len(COPIES)):
@@ -416,8 +431,8 @@
         out[:, lanes] = (xs[own_rows, lanes].astype(jnp.float32) + (mine[k] + come[k])).astype(jnp.bfloat16)
     for k in range(8):
         leaving(k).wait_send()
-    for i in range(len(COPIES)):
-        transfer(i).wait_send()
+    for _, i in sending:
+        waiting(i).wait_send()
 
 
 def rope_tables():
@@ -438,7 +453,7 @@
     bf16, f32 = jnp.bfloat16, jnp.float32
     n = len(COPIES)
     dma = pltpu.SemaphoreType.DMA
-    anywhere = pl.BlockSpec(memory_space=pl.ANY)
+    anywhere = pl.BlockSpec(memory_space=pltpu.HBM)
     inside = pl.BlockSpec(memory_space=pltpu.VMEM)
     return pl.pallas_call(
         kernel,
@@ -462,20 +477,21 @@
             vmem((4, 2 * SEQ, 128), bf16),
             vmem((4, 2 * SEQ, 128), bf16),
             vmem((4, 2 * SEQ, 128), bf16),
-            vmem((4, SEQ, SEQ), f32),
-            vmem((2, SEQ, 2 * SEQ), bf16),
+            vmem((8, SEQ, SEQ), f32),
+            vmem((4, SEQ, 2 * SEQ), bf16),
             vmem((2 * SEQ, 1024), bf16),
             vmem((8, 2 * SEQ, 256), f32),
             vmem((8, SEQ, 256), f32),
             vmem((8, SEQ, 256), f32),
             vmem((8, SEQ, 256), f32),
-            dma((11,)), dma((9,)), dma((9,)), dma((n,)), dma((n,)), dma((8,)), dma((8,)),
+            vmem((8, 2560), bf16),
+            dma((11,)), dma((7,)), dma((9,)), dma((9,)), dma((n,)), dma((n,)), dma((8,)), dma((8,)),
         ],
         compiler_params=pltpu.CompilerParams(
-            collective_id=0, has_side_effects=True, vmem_limit_bytes=60 * 2**20
+            collective_id=0, has_side_effects=True, vmem_limit_bytes=40 * 2**20
         ),
         name="attention_block",
-    )(hidden, spread, wq, wk, wv, w_out.T, cos, sin)
+    )(*(pltpu.with_memory_space_constraint(a, pltpu.HBM) for a in (hidden, spread, wq, wk, wv, w_out.T, cos, sin)))
 
 
 def solution(mesh):

time: 75.3 us -> 71.5 us (0.950)
  Pallas kernels: 71.6 us -> 69.1 us
  local copies, waits for them, and re-layouts: 3.05 us -> 1.72 us
    pallas_call x1, Pallas kernels: 71.6 us -> 69.1 us  [body(): pl.pallas_call(kernel, out_shape=jax.ShapeDtypeStruct((SEQ, D), bf16), in...]
    unnamed x3, local copies, waits for them, and re-layouts: 2.96 us -> 1.63 us
where the time goes in v3:
time: 71.5 us; the launch traced here: 71.4 us
  Pallas kernels  69.1 us (97%)
  local copies, waits for them, and re-layouts  1.72 us (2%)
    pallas_call x1, Pallas kernels, body(): pl.pallas_call(kernel, out_shape=jax.ShapeDtypeStruct((SEQ, D), bf16), in...  69.1 us
    unnamed x3, local copies, waits for them, and re-layouts  1.63 us

profile of v3, /device:TPU:1, one launch (start us, length us, event | category | flops | bytes accessed | tf_op | source)
XLA Modules:
  0.0 71.4 jit_solution(14271804651351245828)
XLA Ops:
  0.0 0.0 copy-start
  0.0 0.7 copy-done
  0.7 0.1 tile.10
  0.7 0.5 compare_select_fusion.gain
  1.3 69.1 %attention_block.1 = bf16[256,2048]{1,0:T(8,128)(2,1)S(1)} custom-call(bf16[256,2048]{1,0:T(8,128)(2,1)} %hidden.1, f32[1,128]{1,0:T(1,128)} %compare_select_fusion.gain, bf16[8,2048]{1,0:T(8,128)(2,1)} %wq.1, bf16[8,512]{1,0:T(8,128)(2,1)} %wk.1, bf16[8,512]{1,0:T(8,128)(2,1)} %wv.1, bf16[8,2048]{1,0:T(8,128)(2,1)} %bitcast.1, ...), custom_call_target="tpu_custom_call" | custom-call | tf_op jit(solution)/shard_map/attention_block/pallas_call | solution.py:458
  70.4 1.0 %copy.10 = bf16[256,2048]{1,0:T(8,128)(2,1)} copy(bf16[256,2048]{1,0:T(8,128)(2,1)S(1)} %attention_block.1) | data formatting | bytes 2097152
  (1 shorter events, 0.0 us)
Async XLA Ops:
  0.0 0.7 copy-start

commit v4 on v3

--- a/solution.py
+++ b/solution.py
@@ -1,5 +1,3 @@
-import math
-
 import jax
 import jax.numpy as jnp
 import numpy as np
@@ -20,7 +18,7 @@
 LANES = {"X": {"p": 512, "o": 384}, "Y": {"p": 512, "o": 256}, "Z": {"p": 512, "o": 384}, "G": {"g": 32}}
 GROUPS = {8: ((0, 1), (1, 2), (3, 2), (5, 3)), 4: ((0, 1), (1, 2), (3, 1))}
 RANK = {"g": (-1, -1, -1), "p": (0, 1, 3), "o": (1, 3, 7)}
-RATE, LATENCY, ISSUE, BEGIN = 46.6e3, 2.2, 0.1, 4.0
+RATE, LATENCY, ISSUE, BEGIN = 46.6e3, 2.3, 0.1, 5.5
 
 
 def slot(n, step, way):
@@ -111,7 +109,7 @@
     hidden, gain, wq, wk, wv, wo, cos_in, sin_in, out,
     px, py, pz, ox, oy, oz, sg, xs, cos, sin, normed, q_all, k_lo, k_hi, v_lo, v_hi,
     score, prob, ctx, acc, mine, gone, come,
-    stage, local, staged, away, here, sent, got, out_sent, out_got,
+    stage, few, local, staged, away, here, sent, got, out_sent, out_got,
 ):
     f, r = lax.axis_index("fsdp"), lax.axis_index("rep")
     at = {"z": f // 4, "y": f % 4, "x": r // 2}
@@ -150,9 +148,13 @@
         ):
             _, b, c = (at[axis] for axis in ORDER[name[0]])
             yield source, buffers[name].at[c, b, 0, rows, pl.ds(lane, source.shape[1])]
-        yield gain, sg.at[at["z"], at["y"], 0, core]
+        if t is other:
+            yield own_gain, own_gain
         yield hidden, xs.at[own_rows]
 
+    own_gain = sg.at[at["z"], at["y"], 0, core]
+    taking = pltpu.make_async_copy(gain, few, staged.at[7])
+    taking.start()
     starting = []
     for i, (source, target) in enumerate(shares(core)):
         starting.append(pltpu.make_async_copy(source, target, local.at[i]))
@@ -169,6 +171,10 @@
     ]
     for copy in tables:
         copy.start()
+    taking.wait()
+    spread = jnp.concatenate([few[...].astype(jnp.float32).reshape(1, 8)] * 16, axis=1)
+    place = lax.broadcasted_iota(jnp.int32, (1, 128), 1) // 8
+    sg[at["z"], at["y"], 0, core] = jnp.where(place == f % 2 * 8 + r, spread, 0.0)
     pl.semaphore_wait(barrier, len(peers))
     for i, (source, target) in enumerate(shares(other)):
         if i < 7:
@@ -180,8 +186,7 @@
         )
         copy.start()
         starting.append(copy)
-    count = len(starting) // 2
-    for copy in starting[: count - 1] + starting[count : 2 * count - 1]:
+    for copy in starting[:7] + starting[8:16]:
         copy.wait()
 
     def halves(n, half):
@@ -294,6 +299,10 @@
                     piece * HD**-0.5
                 ).astype(jnp.bfloat16)
 
+    def project_two(name, start):
+        project_q(name, 0, start)
+        project_q(name, 256, start + 256)
+
     def project_kv(lo, turn, low, high):
         t = dot(normed[...], columns("Zp", lo, 256))
         for s in range(2):
@@ -350,6 +359,10 @@
         )
         acc[z] = dot_t(ctx[:, :640], weights)
 
+    def mix_two(z):
+        mix_first(z)
+        mix_first(z + 1)
+
     def chunk_of(k):
         step, way = FAR[k]
         return (at["z"] - way * step + 8) % 8
@@ -371,11 +384,11 @@
 
     def work(parts, cost, run, *args, needs=()):
         needs = list(needs) + [i for part in parts for i in PART[part]]
-        works.append((max(COME[i] for i in needs), cost * 0.6, needs, run, args))
+        works.append((max(COME[i] for i in needs), cost * 0.7, needs, run, args))
 
     def prepare():
-        starting[count - 1].wait()
-        starting[2 * count - 1].wait()
+        starting[7].wait()
+        starting[16].wait()
         for copy in tables:
             copy.wait()
         for pair in range(4):
@@ -388,14 +401,13 @@
     work([("Z", "p")], 0.8, project_kv, 0, True, k_lo, k_hi)
     work([("Z", "p")], 0.8, project_kv, 256, False, v_lo, v_hi)
     for name, start in (("X", 0), ("Y", 512)):
-        for lo in (0, 256):
-            work([(name, "p")], 0.8, project_q, name + "p", lo, start + lo)
+        work([(name, "p")], 1.4, project_two, name + "p", start)
     works[5:] = sorted(works[5:], key=lambda w: w[0])
     for name, heads in (("X", (0, 1)), ("Y", (2, 3))):
         for head in heads:
             work([(name, "p"), ("Z", "p")], 1.7, attend_both, head)
-    for z in range(8):
-        work([("X", "o"), ("Y", "o")], 0.4, mix_first, z)
+    for z in range(0, 8, 2):
+        work([("X", "o"), ("Y", "o")], 0.9, mix_two, z)
     for k in range(8):
         work([], 0.3, mix_last, k, needs=LAST[FAR[k]] if k else [i for i in PART["Z", "o"] if COPIES[i][0][2] < 2])
 
@@ -446,9 +458,6 @@
 
 def body(hidden, gain, wq, wk, wv, w_out):
     cos, sin = rope_tables()
-    device = lax.axis_index("fsdp") * 8 + lax.axis_index("rep")
-    spread = jnp.tile(gain.astype(jnp.float32), 16)
-    spread = jnp.where(jnp.arange(128) // 8 == device % 16, spread, 0.0)[None, :]
     vmem = pltpu.VMEM
     bf16, f32 = jnp.bfloat16, jnp.float32
     n = len(COPIES)
@@ -485,13 +494,14 @@
             vmem((8, SEQ, 256), f32),
             vmem((8, SEQ, 256), f32),
             vmem((8, 2560), bf16),
-            dma((11,)), dma((7,)), dma((9,)), dma((9,)), dma((n,)), dma((n,)), dma((8,)), dma((8,)),
+            vmem((8,), bf16),
+            dma((11,)), dma((8,)), dma((9,)), dma((9,)), dma((n,)), dma((n,)), dma((8,)), dma((8,)),
         ],
         compiler_params=pltpu.CompilerParams(
             collective_id=0, has_side_effects=True, vmem_limit_bytes=40 * 2**20
         ),
         name="attention_block",
-    )(*(pltpu.with_memory_space_constraint(a, pltpu.HBM) for a in (hidden, spread, wq, wk, wv, w_out.T, cos, sin)))
+    )(*(pltpu.with_memory_space_constraint(a, pltpu.HBM) for a in (hidden, gain, wq, wk, wv, w_out.T, cos, sin)))
 
 
 def solution(mesh):

time: 71.5 us -> 69.6 us (0.973)
  local copies, waits for them, and re-layouts: 1.72 us -> 0.97 us
    unnamed x3 -> x1, local copies, waits for them, and re-layouts: 1.63 us -> 0.97 us
where the time goes in v4:
time: 69.6 us; the launch traced here: 69.5 us
  Pallas kernels  68.5 us (98%)
  local copies, waits for them, and re-layouts  0.97 us (1%)
    pallas_call x1, Pallas kernels, body(): pl.pallas_call(kernel, out_shape=jax.ShapeDtypeStruct((SEQ, D), bf16), in...  68.5 us

profile of v4, /device:TPU:1, one launch (start us, length us, event | category | flops | bytes accessed | tf_op | source)
XLA Modules:
  0.0 69.5 jit_solution(9514050910231412844)
XLA Ops:
  0.0 68.5 %attention_block.1 = bf16[256,2048]{1,0:T(8,128)(2,1)S(1)} custom-call(bf16[256,2048]{1,0:T(8,128)(2,1)} %hidden.1, bf16[8]{0:T(256)(128)(2,1)} %gain.1, bf16[8,2048]{1,0:T(8,128)(2,1)} %wq.1, bf16[8,512]{1,0:T(8,128)(2,1)} %wk.1, bf16[8,512]{1,0:T(8,128)(2,1)} %wv.1, bf16[8,2048]{1,0:T(8,128)(2,1)} %bitcast.1, f32[256,128]{1,0:T(8,128)} %constant.4.clone.cos_in, ...), custom_call_target="tpu_custom_call" | custom-call | tf_op jit(solution)/shard_map/attention_block/pallas_call | solution.py:467
  68.5 1.0 %copy.10 = bf16[256,2048]{1,0:T(8,128)(2,1)} copy(bf16[256,2048]{1,0:T(8,128)(2,1)S(1)} %attention_block.1) | data formatting | bytes 2097152

commit v5 on v4

--- a/solution.py
+++ b/solution.py
@@ -155,16 +155,16 @@
     own_gain = sg.at[at["z"], at["y"], 0, core]
     taking = pltpu.make_async_copy(gain, few, staged.at[7])
     taking.start()
-    starting = []
-    for i, (source, target) in enumerate(shares(core)):
-        starting.append(pltpu.make_async_copy(source, target, local.at[i]))
-        starting[-1].start()
     widths = [source.shape[1] for source, _ in list(shares(other))[:7]]
     kept = [stage.at[:, pl.ds(sum(widths[:i]), width)] for i, width in enumerate(widths)]
     staging = []
     for i, (source, _) in enumerate(list(shares(other))[:7]):
         staging.append(pltpu.make_async_copy(source, kept[i], staged.at[i]))
         staging[-1].start()
+    starting = []
+    for i, (source, target) in enumerate(shares(core)):
+        starting.append(pltpu.make_async_copy(source, target, local.at[i]))
+        starting[-1].start()
     tables = [
         pltpu.make_async_copy(cos_in, cos, local.at[9]),
         pltpu.make_async_copy(sin_in, sin, local.at[10]),

time: 69.6 us -> 69.6 us (level)
  no operation moved by 1% of the time
where the time goes in v5:
time: 69.6 us; the launch traced here: 69.5 us
  Pallas kernels  68.5 us (98%)
  local copies, waits for them, and re-layouts  0.97 us (1%)
    pallas_call x1, Pallas kernels, body(): pl.pallas_call(kernel, out_shape=jax.ShapeDtypeStruct((SEQ, D), bf16), in...  68.5 us

profile of v5, /device:TPU:1, one launch (start us, length us, event | category | flops | bytes accessed | tf_op | source)
XLA Modules:
  0.0 69.5 jit_solution(4320054478269921986)
XLA Ops:
  0.0 68.5 %attention_block.1 = bf16[256,2048]{1,0:T(8,128)(2,1)S(1)} custom-call(bf16[256,2048]{1,0:T(8,128)(2,1)} %hidden.1, bf16[8]{0:T(256)(128)(2,1)} %gain.1, bf16[8,2048]{1,0:T(8,128)(2,1)} %wq.1, bf16[8,512]{1,0:T(8,128)(2,1)} %wk.1, bf16[8,512]{1,0:T(8,128)(2,1)} %wv.1, bf16[8,2048]{1,0:T(8,128)(2,1)} %bitcast.1, f32[256,128]{1,0:T(8,128)} %constant.4.clone.cos_in, ...), custom_call_target="tpu_custom_call" | custom-call | tf_op jit(solution)/shard_map/attention_block/pallas_call | solution.py:467
  68.5 1.0 %copy.10 = bf16[256,2048]{1,0:T(8,128)(2,1)} copy(bf16[256,2048]{1,0:T(8,128)(2,1)S(1)} %attention_block.1) | data formatting | bytes 2097152
